TPU v7x, 512 devices: a whole 4x8x8 slice. The times are simulated.
512 devices in a mesh: dp: 64 (over x, z, core), mp: 8 (over y).
Axes of the slice: x: 4, y: 8, z: 8, core: 2. Of those that a mesh axis runs over, the one named last changes fastest.
Arguments:
- node_feats: bfloat16 [256, 131072], P('mp', 'dp'), may hold values from -6 to 6
- proj_weight: bfloat16 [256, 256], P('mp'), may hold values from -0.375 to 0.375
- att_src: float32 [256], P('mp'), may hold values from -32 to 32
- att_dst: float32 [256], P('mp'), may hold values from -32 to 32
- out_bias: float32 [256], P('mp'), may hold values from -3 to 3
- tile_rows: int32 [2048], P('dp'), may hold values from 0 to 1023, as said below
- tile_cols: int32 [2048], P('dp'), may hold values from 0 to 1023, as said below
- tile_masks: int32 [2048, 4, 128], P('dp'), may hold values from -2147483648 to 2147483646
Outputs:
- node_out: bfloat16 [256, 131072], P('mp', 'dp')
Inputs may be any that keep to these rules, and one draw needn't show every extreme that they name: `tile_rows`: block b holds nodes 128 b to 128 b + 127 and belongs to index b // 16 of dp. Among the 32 tiles of one index of dp, no owner's blocks are named more than 2 times; on every index one owner's blocks are named exactly 2 times. `tile_cols`: the same bound holds for source blocks: among the 32 tiles of one index of dp, no owner's blocks are named more than 2 times, and one owner's exactly 2 times on every index.
All inputs are finite; a program needn't handle non-finite values.
Results may differ from a plain program's by a relative error of at most 0.0034.
Values may be sent and summed in bfloat16 or wider, within the bound.
A program may use at most 64 MiB of HBM per device.

v0:
```python
import math

import jax
import jax.numpy as jnp
from jax import lax
from jax.sharding import PartitionSpec as P

HD = 32


far_below = -1e30


def in_order(pieces, dim):
    pieces = jnp.moveaxis(pieces, 0, dim)
    shape = pieces.shape
    return pieces.reshape(*shape[:dim], shape[dim] * shape[dim + 1], *shape[dim + 2 :])


def from_everyone(value, axis):
    length = lax.axis_size(axis)
    return lax.all_to_all(
        jnp.broadcast_to(value[None], (length, *value.shape)), axis, 0, 0, tiled=True
    )


def collect(value, axis, dim):
    return in_order(from_everyone(value, axis), dim)


def side_by_side(arrays, axis, split_dim, concat_dim, along):
    both = jnp.concatenate(arrays, axis=along)
    result, at, outs = (
        lax.all_to_all(both, axis, split_axis=split_dim, concat_axis=concat_dim, tiled=True),
        0,
        [],
    )
    for a in arrays:
        outs.append(lax.slice_in_dim(result, at, at + a.shape[along], axis=along))
        at += a.shape[along]
    return tuple(outs)


def side_by_side_2(arrays, axis, split_dim, concat_dim, along):
    columns = [a.reshape(*a.shape[:along], -1) for a in arrays]
    both = jnp.concatenate(columns, axis=along)
    result, at, outs = (
        lax.all_to_all(both, axis, split_axis=split_dim, concat_axis=concat_dim, tiled=True),
        0,
        [],
    )
    for a, column in zip(arrays, columns):
        share = result[..., at : at + column.shape[along]]
        outs.append(share.reshape(*share.shape[:along], *a.shape[along:]))
        at += column.shape[along]
    return tuple(outs)


def leaky_relu(scores):
    return jnp.where(scores > 0, scores, 0.2 * scores)


def unpack_bits(packed):
    offsets = jnp.arange(32, dtype=jnp.int32)
    spread = jnp.bitwise_and(jnp.right_shift(packed[..., :, None, :], offsets[:, None]), 1)
    return spread.reshape(packed.shape[:-2] + (packed.shape[-2] * 32, packed.shape[-1]))


def edge_scores(edge_mask, source, target):
    raw_scores = leaky_relu(target[:, :, None, :] + source[:, :, :, None])
    return jnp.where(edge_mask[:, None] == 1, raw_scores, far_below)


def tile_group(inputs):
    packed, feats_here, source_here, target_here = inputs
    edge_mask = unpack_bits(packed)
    scores = edge_scores(edge_mask, source_here, target_here)
    tile_peaks = jnp.max(scores, axis=2)
    weights = jnp.where(edge_mask[:, None] == 1, jnp.exp(scores - tile_peaks[:, :, None, :]), 0.0)
    masses = jnp.sum(weights, axis=2)
    values = jnp.einsum(
        "ghdc,ghcr->ghdr",
        feats_here,
        weights.astype(jnp.bfloat16),
        preferred_element_type=jnp.float32,
    )
    return (tile_peaks, masses, values)


def local(node_feats, proj_weight, att_src, att_dst, out_bias, tile_rows, tile_cols, tile_masks):
    local_rows = node_feats.shape[1]
    head_dims = proj_weight.shape[0]
    local_heads = head_dims // HD
    tile_size = tile_masks.shape[2]
    local_blocks = local_rows // tile_size
    tile_count = tile_rows.shape[0]
    devices_dp = lax.axis_size("dp")
    capacity = max(2, 2 * tile_count // devices_dp)
    slot_count = devices_dp * capacity
    projected = jnp.dot(
        proj_weight, collect(node_feats, "mp", 0), preferred_element_type=jnp.float32
    )
    features = projected.astype(jnp.bfloat16)
    by_head = projected.reshape(local_heads, HD, local_rows)
    source = jnp.einsum(
        "hd,hdn->hn", att_src.reshape(local_heads, HD), by_head, precision=lax.Precision.HIGHEST
    )
    target = jnp.einsum(
        "hd,hdn->hn", att_dst.reshape(local_heads, HD), by_head, precision=lax.Precision.HIGHEST
    )
    source_blocks = source.reshape(local_heads, local_blocks, tile_size).transpose(1, 0, 2)
    target_blocks = target.reshape(local_heads, local_blocks, tile_size).transpose(1, 0, 2)
    feat_blocks = features.reshape(local_heads, HD, local_blocks, tile_size).transpose(2, 0, 1, 3)

    def slots_of(block_ids):
        owners = block_ids // local_blocks
        position = jnp.arange(tile_count, dtype=jnp.int32)
        earlier = (owners[:, None] == owners[None, :]) & (position[None, :] < position[:, None])
        return (owners * capacity + jnp.sum(earlier, axis=1), block_ids % local_blocks)

    def to_slots(slot_ids, entries):
        slot_hits = slot_ids[:, None] == jnp.arange(slot_count, dtype=jnp.int32)[None, :]
        return jnp.sum(jnp.where(slot_hits, entries[:, None], 0), axis=0).reshape(
            devices_dp, capacity
        )

    col_slot, col_local = slots_of(tile_cols)
    row_slot, row_local = slots_of(tile_rows)
    col_wanted = to_slots(col_slot, col_local)
    wanted, wanted_rows = side_by_side((col_wanted, to_slots(row_slot, row_local)), "dp", 0, 0, 1)
    send_source = jnp.take(source_blocks, wanted.reshape(-1), axis=0).reshape(
        devices_dp, capacity, local_heads, tile_size
    )
    send_target = jnp.take(target_blocks, wanted_rows.reshape(-1), axis=0).reshape(
        devices_dp, capacity, local_heads, tile_size
    )
    got_source, got_target = side_by_side((send_source, send_target), "dp", 0, 0, 1)
    tile_source = jnp.take(got_source.reshape(slot_count, local_heads, tile_size), col_slot, axis=0)
    tile_target = jnp.take(got_target.reshape(slot_count, local_heads, tile_size), row_slot, axis=0)
    send_feats = jnp.take(feat_blocks, wanted.reshape(-1), axis=0).reshape(
        devices_dp, capacity, local_heads, HD, tile_size
    )
    got_feats = lax.all_to_all(send_feats, "dp", split_axis=0, concat_axis=0, tiled=True)
    tile_feats = jnp.take(
        got_feats.reshape(slot_count, local_heads, HD, tile_size), col_slot, axis=0
    )
    group_size = math.gcd(tile_count, 8)

    def grouped(stacked):
        return stacked.reshape((tile_count // group_size, group_size) + stacked.shape[1:])

    tile_peaks, masses, values = lax.map(
        tile_group,
        (grouped(tile_masks), grouped(tile_feats), grouped(tile_source), grouped(tile_target)),
    )
    tile_peaks = tile_peaks.reshape(tile_count, local_heads, tile_size)
    masses = masses.reshape(tile_count, local_heads, tile_size)
    values = values.reshape(tile_count, local_heads, HD, tile_size)
    slot_hits = row_slot[:, None] == jnp.arange(slot_count, dtype=jnp.int32)[None, :]
    filled = jnp.any(slot_hits, axis=0)
    source_tile = jnp.sum(
        jnp.where(slot_hits, jnp.arange(tile_count, dtype=jnp.int32)[:, None], 0), axis=0
    )
    send_values = jnp.where(
        filled[:, None, None, None], jnp.take(values, source_tile, axis=0), 0.0
    ).reshape(devices_dp, capacity, local_heads, HD, tile_size)
    send_peaks = jnp.where(
        filled[:, None, None], jnp.take(tile_peaks, source_tile, axis=0), far_below
    ).reshape(devices_dp, capacity, local_heads, tile_size)
    send_masses = jnp.where(
        filled[:, None, None], jnp.take(masses, source_tile, axis=0), 0.0
    ).reshape(devices_dp, capacity, local_heads, tile_size)
    send_codes = (
        jnp.where(filled, jnp.take(row_local, source_tile), 0)
        .astype(jnp.float32)
        .reshape(devices_dp, capacity)
    )
    got_values, got_peaks, got_masses, got_codes = side_by_side_2(
        (send_values, send_peaks, send_masses, send_codes), "dp", 0, 0, 2
    )
    got_values = got_values.reshape(slot_count, local_heads, HD, tile_size)
    got_peaks = got_peaks.reshape(slot_count, local_heads, tile_size)
    got_masses = got_masses.reshape(slot_count, local_heads, tile_size)
    row_codes = got_codes.reshape(slot_count).astype(jnp.int32)
    self_scores = leaky_relu(source_blocks + target_blocks)
    row_peak = self_scores.at[row_codes].max(got_peaks)
    rescale = jnp.exp(got_peaks - row_peak[row_codes])
    self_weight = jnp.exp(self_scores - row_peak)
    denominator = self_weight.at[row_codes].add(rescale * got_masses)
    summed = (
        (self_weight[:, :, None, :] * feat_blocks.astype(jnp.float32))
        .at[row_codes]
        .add(rescale[:, :, None, :] * got_values)
    )
    gathered = summed / denominator[:, :, None, :]
    flat_out = gathered.transpose(1, 2, 0, 3).reshape(head_dims, local_rows)
    return jax.nn.elu(flat_out + node_feats.astype(jnp.float32) + out_bias[:, None]).astype(
        jnp.bfloat16
    )


def solution(mesh):
    return jax.shard_map(
        local,
        mesh=mesh,
        in_specs=(
            P("mp", "dp"),
            P("mp", None),
            P("mp"),
            P("mp"),
            P("mp"),
            P("dp"),
            P("dp"),
            P("dp", None, None),
        ),
        out_specs=P("mp", "dp"),
        check_vma=False,
    )
```

profile of v0, /device:TPU:1, one launch (start us, length us, event | category | flops | bytes accessed | tf_op | source)
XLA Modules:
  0.0 216.7 jit_solution(18003091887082817628)
XLA Ops:
  2.9 14.8 %all-to-all-start.1 = ((s32[64,1,4]{2,1,0:T(1,128)}), s32[64,1,4]{2,1,0:T(1,128)S(1)}, u32[]{:S(2)}, u32[]{:S(2)}) async-start(s32[64,1,4]{2,1,0:T(1,128)} %bitcast.19), calls=%async_computation.1 | async-start | bytes 65536 | tf_op jit(solution)/shard_map/all_to_all | solution.py:34
  18.8 1.2 gather_fusion.3
  20.3 6.7 %all-to-all-done.1 = s32[64,1,4]{2,1,0:T(1,128)S(1)} async-done(((s32[64,1,4]{2,1,0:T(1,128)}), s32[64,1,4]{2,1,0:T(1,128)S(1)}, u32[]{:S(2)}, u32[]{:S(2)}) %all-to-all-start.1) | async-done | bytes 1056 | tf_op jit(solution)/shard_map/all_to_all | solution.py:34
  27.0 2.0 broadcast_in_dim.188
  29.0 7.0 %all-to-all-start = ((bf16[8,32,2048]{2,1,0:T(8,128)(2,1)}), bf16[8,32,2048]{2,1,0:T(8,128)(2,1)S(1)}, u32[]{:S(2)}, u32[]{:S(2)}) async-start(bf16[8,32,2048]{2,1,0:T(8,128)(2,1)} %broadcast_in_dim.188), calls=%async_computation | async-start | bytes 2097152 | tf_op jit(solution)/shard_map/all_to_all | solution.py:22
  36.6 28.6 %all-to-all-done = bf16[8,32,2048]{2,1,0:T(8,128)(2,1)S(1)} async-done(((bf16[8,32,2048]{2,1,0:T(8,128)(2,1)}), bf16[8,32,2048]{2,1,0:T(8,128)(2,1)S(1)}, u32[]{:S(2)}, u32[]{:S(2)}) %all-to-all-start) | async-done | bytes 1048608 | tf_op jit(solution)/shard_map/all_to_all | solution.py:22
  68.2 4.5 %all-to-all-start.2 = ((f32[64,4,1,128]{3,1,2,0:T(4,128)}), f32[64,4,1,128]{3,1,2,0:T(4,128)S(1)}, u32[]{:S(2)}, u32[]{:S(2)}) async-start(f32[64,4,1,128]{3,1,2,0:T(4,128)} %pad_maximum_fusion.1), calls=%async_computation.2 | async-start | bytes 262144 | tf_op jit(solution)/shard_map/all_to_all | solution.py:34
  73.6 1.2 broadcast_select_fusion
  74.8 8.4 %all-to-all-done.2 = f32[64,4,1,128]{3,1,2,0:T(4,128)S(1)} async-done(((f32[64,4,1,128]{3,1,2,0:T(4,128)}), f32[64,4,1,128]{3,1,2,0:T(4,128)S(1)}, u32[]{:S(2)}, u32[]{:S(2)}) %all-to-all-start.2) | async-done | bytes 131104 | tf_op jit(solution)/shard_map/all_to_all | solution.py:34
  83.2 4.9 %all-to-all-start.3 = ((bf16[64,2,1,32,128]{4,3,1,2,0:T(8,128)(2,1)}), bf16[64,2,1,32,128]{4,3,1,2,0:T(8,128)(2,1)S(1)}, u32[]{:S(2)}, u32[]{:S(2)}) async-start(bf16[64,2,1,32,128]{4,3,1,2,0:T(8,128)(2,1)} %broadcast_select_fusion), calls=%async_computation.3 | async-start | bytes 2097152 | tf_op jit(solution)/shard_map/all_to_all | solution.py:143
  89.6 27.0 %all-to-all-done.3 = bf16[64,2,1,32,128]{4,3,1,2,0:T(8,128)(2,1)S(1)} async-done(((bf16[64,2,1,32,128]{4,3,1,2,0:T(8,128)(2,1)}), bf16[64,2,1,32,128]{4,3,1,2,0:T(8,128)(2,1)S(1)}, u32[]{:S(2)}, u32[]{:S(2)}) %all-to-all-start.3) | async-done | bytes 1048608 | tf_op jit(solution)/shard_map/all_to_all | solution.py:143
  117.3 8.0 %while.14 = (s32[]{:T(128)}, f32[4,8,1,128]{3,1,2,0:T(8,128)S(1)}, f32[4,8,1,128]{3,2,1,0:T(1,128)S(1)}, f32[4,8,1,32,128]{4,3,1,2,0:T(8,128)S(1)}, s32[4,8,4,12...) while((s32[]{:T(128)}, f32[4,8,1,128]{3,1,2,0:T(8,128)S(1)}, ...), condition=%wide.region_9.12_spmd, body=%wide.region_6.11_spmd.sunk | while | flops 12449794 | bytes 896117 | solution.py:152
  125.4 2.1 gather_fusion.2
  127.5 2.4 %gather.43 = f32[64,2,4096]{2,1,0:T(2,128)S(1)} reshape(f32[128,32,128]{2,1,0:T(8,128)} %gather_fusion.2) | data formatting | bytes 4194304 | tf_op jit(solution)/shard_map/jit(_take)/gather | solution.py:165
  131.2 2.4 %select_select_fusion = f32[64,2,4096]{2,1,0:T(2,128)S(1)} fusion(f32[64,2,4096]{2,1,0:T(2,128)S(1)} %gather.43, pred[64,2]{1,0:T(8,128)(4,1)S(1)} %compare_and_fusion.1, pred[64,2]{1,0:T(8,128)(4,1)S(1)} %broadcast_in_dim.189), kind=kLoop, calls=%fused_computation.40 | loop fusion | flops 1048576 | bytes 4194560 | tf_op jit(solution)/shard_map/jit(_where)/select_n | solution.py:164
  133.6 2.2 %pad_maximum_fusion = f32[64,2,4353]{2,1,0:T(2,128)} fusion(f32[64,2,1]{2,1,0:T(2,128)S(1)} %fusion.26, f32[64,2,128]{2,1,0:T(2,128)S(1)} %bitcast.217, f32[64,2,128]{2,1,0:T(2,128)S(1)} %bitcast.216, f32[64,2,4096]{2,1,0:T(2,128)S(1)} %select_select_fusion), kind=kLoop, calls=%fused_computation.38 | loop fusion | flops 1671552 | bytes 4457472 | tf_op jit(solution)/shard_map/concatenate | solution.py:46
  135.9 6.4 %all-to-all-start.4 = ((f32[64,2,4353]{2,1,0:T(2,128)}), f32[64,2,4353]{2,1,0:T(2,128)S(1)}, u32[]{:S(2)}, u32[]{:S(2)}) async-start(f32[64,2,4353]{2,1,0:T(2,128)} %pad_maximum_fusion), calls=%async_computation.4 | async-start | bytes 4587520 | tf_op jit(solution)/shard_map/all_to_all | solution.py:48
  142.3 55.2 %all-to-all-done.4 = f32[64,2,4353]{2,1,0:T(2,128)S(1)} async-done(((f32[64,2,4353]{2,1,0:T(2,128)}), f32[64,2,4353]{2,1,0:T(2,128)S(1)}, u32[]{:S(2)}, u32[]{:S(2)}) %all-to-all-start.4) | async-done | bytes 2228768 | tf_op jit(solution)/shard_map/all_to_all | solution.py:48
  198.9 1.3 scatter_fusion
  200.8 1.6 slice.60
  202.5 4.0 %reshape_reshape.24 = f32[128,1,32,128]{3,2,0,1:T(8,128)} reshape(f32[64,2,4096]{2,1,0:T(2,128)} %slice.60) | data formatting | bytes 4194304 | tf_op jit(solution)/shard_map/reshape;reshape | solution.py:181
  206.5 1.9 multiply_bitcast_fusion
  208.4 5.9 %scatter_fusion.1 = f32[16,32,128]{2,1,0:T(8,128)S(1)} fusion(f32[16,32,128]{2,1,0:T(8,128)S(1)} %multiply_bitcast_fusion.1, s32[128]{0:T(128)S(1)} %fusion.37, f32[128,32,128]{2,1,0:T(8,128)S(1)} %multiply_bitcast_fusion), kind=kCustom, calls=%fused_computation.12 | custom fusion | flops 524288 | bytes 6291968 | tf_op jit(solution)/shard_map/scatter-add | solution.py:193
  214.4 1.3 scatter_custom_fusion.2
  (141 shorter events, 22.9 us)
Async XLA Ops:
  0.0 65.1 %copy-start = (bf16[32,256]{1,0:T(8,128)(2,1)S(1)}, bf16[32,256]{1,0:T(8,128)(2,1)}, u32[]{:S(2)}) copy-start(bf16[32,256]{1,0:T(8,128)(2,1)} %param.17) | copy-start | bytes 49156
  2.9 24.1 %all-to-all-start.1 = ((s32[64,1,4]{2,1,0:T(1,128)}), s32[64,1,4]{2,1,0:T(1,128)S(1)}, u32[]{:S(2)}, u32[]{:S(2)}) async-start(s32[64,1,4]{2,1,0:T(1,128)} %bitcast.19), calls=%async_computation.1 | async-start | bytes 65536 | tf_op jit(solution)/shard_map/all_to_all | solution.py:34
  29.0 36.5 %copy-start.2 = (f32[32]{0:T(128)S(1)}, f32[32]{0:T(128)}, u32[]{:S(2)}) copy-start(f32[32]{0:T(128)} %param.18) | copy-start | bytes 388
  29.0 36.7 %copy-start.3 = (f32[32]{0:T(128)S(1)}, f32[32]{0:T(128)}, u32[]{:S(2)}) copy-start(f32[32]{0:T(128)} %param.19) | copy-start | bytes 388
  29.0 36.1 %all-to-all-start = ((bf16[8,32,2048]{2,1,0:T(8,128)(2,1)}), bf16[8,32,2048]{2,1,0:T(8,128)(2,1)S(1)}, u32[]{:S(2)}, u32[]{:S(2)}) async-start(bf16[8,32,2048]{2,1,0:T(8,128)(2,1)} %broadcast_in_dim.188), calls=%async_computation | async-start | bytes 2097152 | tf_op jit(solution)/shard_map/all_to_all | solution.py:22
  68.2 15.0 %all-to-all-start.2 = ((f32[64,4,1,128]{3,1,2,0:T(4,128)}), f32[64,4,1,128]{3,1,2,0:T(4,128)S(1)}, u32[]{:S(2)}, u32[]{:S(2)}) async-start(f32[64,4,1,128]{3,1,2,0:T(4,128)} %pad_maximum_fusion.1), calls=%async_computation.2 | async-start | bytes 262144 | tf_op jit(solution)/shard_map/all_to_all | solution.py:34
  83.2 33.4 %all-to-all-start.3 = ((bf16[64,2,1,32,128]{4,3,1,2,0:T(8,128)(2,1)}), bf16[64,2,1,32,128]{4,3,1,2,0:T(8,128)(2,1)S(1)}, u32[]{:S(2)}, u32[]{:S(2)}) async-start(bf16[64,2,1,32,128]{4,3,1,2,0:T(8,128)(2,1)} %broadcast_select_fusion), calls=%async_computation.3 | async-start | bytes 2097152 | tf_op jit(solution)/shard_map/all_to_all | solution.py:143
  135.9 61.6 %all-to-all-start.4 = ((f32[64,2,4353]{2,1,0:T(2,128)}), f32[64,2,4353]{2,1,0:T(2,128)S(1)}, u32[]{:S(2)}, u32[]{:S(2)}) async-start(f32[64,2,4353]{2,1,0:T(2,128)} %pad_maximum_fusion), calls=%async_computation.4 | async-start | bytes 4587520 | tf_op jit(solution)/shard_map/all_to_all | solution.py:48
  208.4 7.4 %copy-start.1 = (bf16[32,2048]{1,0:T(8,128)(2,1)S(1)}, bf16[32,2048]{1,0:T(8,128)(2,1)}, u32[]{:S(2)}) copy-start(bf16[32,2048]{1,0:T(8,128)(2,1)} %param.16) | copy-start | bytes 393220
  208.4 7.4 %copy-start.4 = (f32[32]{0:T(128)S(1)}, f32[32]{0:T(128)}, u32[]{:S(2)}) copy-start(f32[32]{0:T(128)} %param.20) | copy-start | bytes 388
where the time goes:
time: 218 us; the launch traced here: 217 us
  waiting for transfers between devices  126 us (58%)
  starting transfers between devices  37.6 us (17%)
  other arithmetic  25.7 us (12%)
  local copies, waits for them, and re-layouts  25.2 us (12%)
    all_to_all x1, waiting for transfers between devices, side_by_side_2(): lax.all_to_all(both, axis, split_axis=split_dim, concat_axis=concat_dim,...  55.2 us
    all_to_all x1, waiting for transfers between devices, from_everyone(): lax.all_to_all(jnp.broadcast_to(value[None], (length, *value.shape)), axi...  28.6 us
    all_to_all x1, waiting for transfers between devices, local(): lax.all_to_all(send_feats, 'dp', split_axis=0, concat_axis=0, tiled=True)  27 us
    all_to_all x2, starting transfers between devices, side_by_side(): lax.all_to_all(both, axis, split_axis=split_dim, concat_axis=concat_dim,...  19.4 us
    all_to_all x2, waiting for transfers between devices, side_by_side(): lax.all_to_all(both, axis, split_axis=split_dim, concat_axis=concat_dim,...  15.1 us
    all_to_all x1, starting transfers between devices, from_everyone(): lax.all_to_all(jnp.broadcast_to(value[None], (length, *value.shape)), axi...  6.95 us
    all_to_all x1, starting transfers between devices, side_by_side_2(): lax.all_to_all(both, axis, split_axis=split_dim, concat_axis=concat_dim,...  6.38 us
    scatter-add x1, other arithmetic, local(): summed = (self_weight[:, :, None, :] * feat_blocks.astype(jnp.float32)).a...  5.9 us
  transfers between devices with their start and end apart: 5, of which 5 were waited for; matrix products, arithmetic and copies ran while one was open for 3% of the time, Pallas kernels for 0%

commit v1 on v0

v1 whole, which is shorter than its diff:
```python
import functools

import jax
import jax.numpy as jnp
from jax import lax
from jax.experimental import pallas as pl
from jax.experimental.pallas import tpu as pltpu
from jax.sharding import PartitionSpec as P

MESH = pl.DeviceIdType.MESH
HD = 32
LANES = 128
LOG2E = 1.4426950408889634
NEG = -1e30
FLOOR = -1e28
NX, NZ, NC = 4, 8, 2
CAP = 2
UNROLL = 4


def split3(v):
    a = v.astype(jnp.bfloat16)
    r = v - a.astype(jnp.float32)
    b = r.astype(jnp.bfloat16)
    c = (r - b.astype(jnp.float32)).astype(jnp.bfloat16)
    return [t.astype(jnp.float32) for t in (a, b, c)]


def rows_of(parts, height, width):
    at = lax.broadcasted_iota(jnp.int32, (height, width), 0)
    out = jnp.zeros((height, width), jnp.float32)
    for i, part in enumerate(parts):
        out = jnp.where(at == i, part, out)
    return out


def wait_bytes(ref, sem):
    pltpu.make_async_copy(ref, ref, sem).wait()


def prep_kernel(nb, rows_ref, cols_ref, mask_ref, slot_ref, code_ref, taken):
    owners = code_ref.shape[0]
    tiles = mask_ref.shape[0]
    code_ref[...] = jnp.full(code_ref.shape, -1, jnp.int32)

    def clear(i, _):
        taken[i] = 0
        return 0

    lax.fori_loop(0, owners, clear, 0)
    lane = lax.broadcasted_iota(jnp.int32, (1, LANES), 1)

    def place(t, _):
        row = rows_ref[t]
        owner = row // nb
        k = taken[owner]
        taken[owner] = k + 1
        slot_ref[owner, k] = mask_ref[t]
        code = (row % nb) + cols_ref[t] * nb
        code_ref[owner] = jnp.where(lane == k, code, code_ref[owner])
        return 0

    lax.fori_loop(0, tiles, place, 0)


def gather_kernel(
    ny, nb, x_ref, w_ref, asrc_ref, adst_ref, slot_ref, code_ref,
    F, S, T4, M4, I4,
    wl, wa, xr, fs, ss, ts,
    one, rf, s_ring, r_ring, s_q, r_q, s_sib, r_sib, s_sibq, r_sibq,
):
    by = nb // ny
    ndp = NX * NZ * NC
    cols = by * LANES
    wr = wl.shape[0]
    dp = lax.axis_index("dp")
    y = lax.axis_index("mp")
    c = dp % NC
    z = (dp // NC) % NZ
    xx = dp // (NC * NZ)
    (SX, RX, SW, RW, SM, RM, SI, RI, SF, SS, RS, ST, RT, STX, RTX, SMX, RMX, SIX, RIX) = [
        one.at[i] for i in range(19)
    ]

    def dev(x_, z_, c_):
        return (x_ * NZ + z_) * NC + c_

    def send(src, dst, ssem, rsem, where):
        pltpu.make_async_remote_copy(
            src_ref=src, dst_ref=dst, send_sem=ssem, recv_sem=rsem,
            device_id=where, device_id_type=MESH,
        ).start()

    barrier = pltpu.get_barrier_semaphore()
    for d in range(1, ny):
        pl.semaphore_signal(barrier, inc=1, device_id={"mp": lax.rem(y + d, ny)}, device_id_type=MESH)

    def greet(j, _):
        pl.semaphore_signal(barrier, inc=1, device_id={"dp": lax.rem(dp + j, ndp)}, device_id_type=MESH)
        return 0

    lax.fori_loop(1, ndp, greet, 0)

    w = w_ref[...]
    fin = w.shape[1]
    att = rows_of(split3(asrc_ref[...]) + split3(adst_ref[...]), 16, HD).astype(jnp.bfloat16)
    v = jnp.dot(att, w, preferred_element_type=jnp.float32) * LOG2E
    vs = v[0:1] + v[1:2] + v[2:3]
    vd = v[3:4] + v[4:5] + v[5:6]
    wl[0:HD, :] = w
    wl[HD:wr, :] = rows_of(split3(vs) + split3(vd), 16, fin).astype(jnp.bfloat16)
    xr[pl.ds(pl.multiple_of(y * HD, HD), HD), :] = x_ref[:, pl.ds(pl.multiple_of(y * cols, cols), cols)]
    wa[y] = wl[...]
    M4[xx, dp] = slot_ref[dp]
    I4[xx, dp] = code_ref[dp]

    pl.semaphore_wait(barrier, ndp - 1 + ny - 1)

    for d in range(1, ny):
        p = lax.rem(y + d, ny)
        send(
            x_ref.at[:, pl.ds(pl.multiple_of(p * cols, cols), cols)],
            xr.at[pl.ds(pl.multiple_of(y * HD, HD), HD), :],
            SX, RX, {"mp": p},
        )
        send(wl, wa.at[y], SW, RW, {"mp": p})

    def send_slots(j, _):
        q = lax.rem(dp + j, ndp)
        xq = q // (NC * NZ)
        send(slot_ref.at[q], M4.at[xq, dp], SM, RM, {"dp": q})
        send(code_ref.at[q], I4.at[xq, dp], SI, RI, {"dp": q})
        return 0

    lax.fori_loop(1, ndp, send_slots, 0)

    wait_bytes(xr.at[pl.ds(0, (ny - 1) * HD)], RX)
    wait_bytes(wa.at[pl.ds(0, ny - 1)], RW)

    own = z * NC + c

    def project(h):
        out = jnp.dot(wa[h], xr[...], preferred_element_type=jnp.float32)
        feats = out[0:HD].astype(jnp.bfloat16)
        s = out[HD : HD + 1] + out[HD + 1 : HD + 2] + out[HD + 2 : HD + 3]
        t = out[HD + 3 : HD + 4] + out[HD + 4 : HD + 5] + out[HD + 5 : HD + 6]
        return feats, s, t

    for d in range(1, ny):
        h = lax.rem(y + d, ny)
        feats, s, t = project(h)
        for k in range(by):
            at = slice(k * LANES, (k + 1) * LANES)
            fs[h, k] = feats[:, at]
            ss[h, k : k + 1, :] = s[:, at]
            ts[h, k : k + 1, :] = t[:, at]
    feats, s, t = project(y)
    for k in range(by):
        at = slice(k * LANES, (k + 1) * LANES)
        F[own * nb + y * by + k] = feats[:, at]
        S[own, y, k : k + 1, :] = s[:, at]
        T4[xx, y, k : k + 1, :] = t[:, at]

    for d in range(1, ny):
        p = lax.rem(y + d, ny)
        send(fs.at[p], F.at[pl.ds(own * nb + y * by, by)], SF, rf.at[d], {"mp": p})
        send(ss.at[p], S.at[own, y], SS, RS, {"mp": p})
        send(ts.at[p], T4.at[xx, y], ST, RT, {"mp": p})

    up = {"dp": dev(xx, lax.rem(z + 1, NZ), c)}
    down = {"dp": dev(xx, lax.rem(z + NZ - 1, NZ), c)}
    sib = {"dp": dev(xx, z, NC - 1 - c)}
    ways = (up, down)
    last = NZ // 2
    order = sorted(range(ny), key=lambda d: min(d, ny - d))

    def owner_of(way, hop):
        zo = lax.rem(z + NZ - hop, NZ) if way == 0 else lax.rem(z + hop, NZ)
        return zo * NC + c

    def piece(o, d):
        return F.at[pl.ds(o * nb + lax.rem(y + ny - d, ny) * by, by)]

    def goes(way, hop, i):
        return hop < last or (hop == last and (i < ny // 2) == (way == 0))

    for i, d in enumerate(order):
        if d:
            wait_bytes(piece(own, d), rf.at[d])
        for way in range(2):
            if goes(way, 1, i):
                send(piece(own, d), piece(own, d), s_ring.at[way, 0, i], r_ring.at[way, 0, i], ways[way])
    wait_bytes(S.at[0, pl.ds(0, ny - 1)], RS)
    for way in range(2):
        send(S.at[own], S.at[own], s_q.at[way, 0], r_q.at[way, 0], ways[way])
    wait_bytes(T4.at[0, pl.ds(0, ny - 1)], RT)
    for j in range(1, NX):
        send(T4.at[xx], T4.at[xx], STX, RTX, {"dp": dev(lax.rem(xx + j, NX), z, c)})

    def share(o, i):
        at = pl.ds(o * nb, nb)
        send(F.at[at], F.at[at], s_sib.at[i], r_sib.at[i], sib)
        send(S.at[o], S.at[o], s_sibq.at[i], r_sibq.at[i], sib)

    share(own, 0)

    wait_bytes(M4.at[0, pl.ds(0, ndp - 1)], RM)
    wait_bytes(I4.at[0, pl.ds(0, ndp - 1)], RI)
    for j in range(1, NX):
        to = {"dp": dev(lax.rem(xx + j, NX), z, c)}
        send(M4.at[xx], M4.at[xx], SMX, RMX, to)
        send(I4.at[xx], I4.at[xx], SIX, RIX, to)

    for hop in range(1, last + 1):
        for i, d in enumerate(order):
            for way in range(2):
                if goes(way, hop, i):
                    o = owner_of(way, hop)
                    wait_bytes(piece(o, d), r_ring.at[way, hop - 1, i])
                    if goes(way, hop + 1, i):
                        send(piece(o, d), piece(o, d), s_ring.at[way, hop, i], r_ring.at[way, hop, i], ways[way])
        for way in range(2):
            if hop < last or way == 0:
                o = owner_of(way, hop)
                wait_bytes(S.at[o], r_q.at[way, hop - 1])
                if hop + 1 < last or (hop + 1 == last and way == 0):
                    send(S.at[o], S.at[o], s_q.at[way, hop], r_q.at[way, hop], ways[way])
                share(o, 2 * hop - 1 + way)

    other = NC - 1 - c
    for i in range(NZ):
        hop, way = (i + 1) // 2, (i + 1) % 2
        zo = lax.rem(z + NZ - hop, NZ) if way == 0 else lax.rem(z + hop, NZ)
        o = (zo if i else z) * NC + other
        wait_bytes(F.at[pl.ds(o * nb, nb)], r_sib.at[i])
        wait_bytes(S.at[o], r_sibq.at[i])
    wait_bytes(T4.at[pl.ds(0, NX - 1)], RTX)
    wait_bytes(M4.at[pl.ds(0, NX - 1)], RMX)
    wait_bytes(I4.at[pl.ds(0, NX - 1)], RIX)

    wait_bytes(xr.at[pl.ds(0, (ny - 1) * HD)], SX)
    wait_bytes(wa.at[pl.ds(0, ny - 1)], SW)
    wait_bytes(M4.at[0, pl.ds(0, ndp - 1)], SM)
    wait_bytes(I4.at[0, pl.ds(0, ndp - 1)], SI)
    wait_bytes(fs.at[pl.ds(0, ny - 1)], SF)
    wait_bytes(ss.at[pl.ds(0, ny - 1)], SS)
    wait_bytes(ts.at[pl.ds(0, ny - 1)], ST)
    wait_bytes(T4.at[pl.ds(0, NX - 1)], STX)
    wait_bytes(M4.at[pl.ds(0, NX - 1)], SMX)
    wait_bytes(I4.at[pl.ds(0, NX - 1)], SIX)
    for hop in range(0, last):
        for way in range(2):
            for i, d in enumerate(order):
                if goes(way, hop + 1, i):
                    wait_bytes(piece(own, d), s_ring.at[way, hop, i])
            if hop + 1 < last or way == 0:
                wait_bytes(S.at[own], s_q.at[way, hop])
    for i in range(NZ):
        wait_bytes(F.at[pl.ds(0, nb)], s_sib.at[i])
        wait_bytes(S.at[0], s_sibq.at[i])


def tile_kernel(nb, F, S, T, M, I, pv_ref, pms_ref, st, lst, acc, mx, tbl, sem):
    dp = lax.axis_index("dp")
    xx = dp // (NC * NZ)
    ncol = F.shape[0]
    nrow = T.shape[0]
    nslot = M.shape[0]
    nh = I.shape[0]

    code = I[...]
    lane = lax.broadcasted_iota(jnp.int32, code.shape, 1)
    row = lax.broadcasted_iota(jnp.int32, code.shape, 0)
    col = code // nb
    active = (code >= 0) & (lane < CAP) & (col // ncol == xx)
    tri = lax.broadcasted_iota(jnp.int32, (nh, nh), 0) >= lax.broadcasted_iota(jnp.int32, (nh, nh), 1)
    flags = active.astype(jnp.float32)
    rank = jnp.dot(
        tri.astype(jnp.float32).astype(jnp.bfloat16), flags.astype(jnp.bfloat16), preferred_element_type=jnp.float32
    )
    totals = jnp.sum(flags, axis=0, keepdims=True)
    lane0 = lax.broadcasted_iota(jnp.int32, (1, LANES), 1)
    before = [jnp.zeros((1, 1), jnp.float32)]
    for k in range(CAP):
        before.append(before[-1] + jnp.sum(jnp.where(lane0 == k, totals, 0.0), axis=1, keepdims=True))
    entry = (row * CAP + lane) + ((code % nb) + (col % ncol) * nb) * nslot
    entry = jnp.where(active, entry, 0)
    chunks = tbl.shape[0] - 1
    want = lane0 + 1
    got = [jnp.zeros((1, LANES), jnp.int32) for _ in range(chunks)]
    for k in range(CAP):
        r = (rank[:, k : k + 1] + before[k]).astype(jnp.int32)
        e = entry[:, k : k + 1]
        r = jnp.where(active[:, k : k + 1], r, 0)
        for j in range(chunks):
            got[j] = got[j] + jnp.sum(jnp.where(r == want + j * LANES, e, 0), axis=0, keepdims=True)
    for j in range(chunks):
        tbl[j] = got[j]
    tbl[chunks] = jnp.broadcast_to(before[CAP], (1, LANES)).astype(jnp.int32)
    copy = pltpu.make_async_copy(tbl, lst, sem)
    copy.start()

    for j in range(ncol // LANES):
        st[j] = S[j * LANES : (j + 1) * LANES, :].T
    acc[...] = jnp.zeros(acc.shape, jnp.float32)
    mx[...] = jnp.full(mx.shape, FLOOR, jnp.float32)
    copy.wait()
    count = lst[chunks, 0, 0]

    sub = lax.broadcasted_iota(jnp.int32, (8, LANES), 0)
    ones = jnp.where(
        lax.broadcasted_iota(jnp.int32, (16, LANES), 0) == 0, 1.0, 0.0
    ).astype(jnp.bfloat16)

    def one_tile(idx):
        e = lst[idx // LANES, 0, idx % LANES]
        slot = e % nslot
        rest = e // nslot
        rb = rest % nb
        cl = rest // nb
        r = (slot // (nslot // NX)) * nb + rb
        bits = jnp.where(idx < count, M[slot], 0)
        scol = st[cl // LANES]
        t = T[r]
        which = jnp.full((8, LANES), cl % LANES, jnp.int32)
        picked = []
        top = jnp.full((8, LANES), NEG, jnp.float32)
        for g in range(LANES // 8):
            word = jnp.broadcast_to(bits[g // 4 : g // 4 + 1, :], (8, LANES))
            up = lax.shift_left(word, 31 - (8 * (g % 4)) - sub)
            s = jnp.take_along_axis(scol[8 * g : 8 * g + 8, :], which, axis=1)
            s = jnp.where(up < 0, s, NEG)
            top = jnp.maximum(top, s)
            picked.append(s)
        m = jnp.max(top, axis=0, keepdims=True) + t
        ref = jnp.maximum(jnp.maximum(m, 0.2 * m), FLOOR)
        weights = []
        for s in picked:
            u = s + t
            weights.append(jnp.exp2(jnp.maximum(u, 0.2 * u) - ref))
        wts = jnp.concatenate(weights, axis=0).astype(jnp.bfloat16)
        lhs = jnp.concatenate([F[cl], ones], axis=0)
        val = jnp.dot(lhs, wts, preferred_element_type=jnp.float32)
        return r, ref, val[0 : HD + 8]

    def step(it, _):
        found = [one_tile(it * UNROLL + u) for u in range(UNROLL)]
        for r, ref, val in found:
            old = mx[r]
            new = jnp.maximum(old, ref)
            acc[r] = acc[r] * jnp.exp2(old - new) + val * jnp.exp2(ref - new)
            mx[r] = new
        return 0

    lax.fori_loop(0, (count + UNROLL - 1) // UNROLL, step, 0)

    def put(r, _):
        a = acc[r]
        pv_ref[r] = a[0:HD].astype(jnp.bfloat16)
        pms_ref[r, 0:1, :] = mx[r]
        pms_ref[r, 1:2, :] = a[HD : HD + 1]
        return 0

    lax.fori_loop(0, nrow, put, 0)


def merge_kernel(nb, F, S, T4, x_ref, b_ref, pv, pms, out_ref, rv, rms, fo, so, to, loc, s_v, r_v, s_m, r_m):
    dp = lax.axis_index("dp")
    c = dp % NC
    z = (dp // NC) % NZ
    xx = dp // (NC * NZ)
    own = z * NC + c
    by = so.shape[1]
    copies = [
        pltpu.make_async_copy(F.at[pl.ds(own * nb, nb)], fo, loc.at[0]),
        pltpu.make_async_copy(S.at[own], so, loc.at[1]),
        pltpu.make_async_copy(T4.at[xx], to, loc.at[2]),
    ]
    for cp in copies:
        cp.start()
    barrier = pltpu.get_barrier_semaphore()
    peers = [lax.rem(xx + j, NX) for j in range(1, NX)]
    for p in peers:
        pl.semaphore_signal(barrier, inc=1, device_id={"dp": (p * NZ + z) * NC + c}, device_id_type=MESH)
    pl.semaphore_wait(barrier, NX - 1)
    sends = []
    for j, p in enumerate(peers):
        at = {"dp": (p * NZ + z) * NC + c}
        for src, dst, ssem, rsem in ((pms, rms, s_m, r_m), (pv, rv, s_v, r_v)):
            cp = pltpu.make_async_remote_copy(
                src_ref=src.at[p], dst_ref=dst.at[j], send_sem=ssem.at[j], recv_sem=rsem.at[j],
                device_id=at, device_id_type=MESH,
            )
            cp.start()
            sends.append(cp)
    for cp in copies:
        cp.wait()
    rowi = lax.broadcasted_iota(jnp.int32, (HD, LANES), 0)
    lanei = lax.broadcasted_iota(jnp.int32, (HD, LANES), 1)
    bias = jnp.sum(jnp.where(rowi == lanei, b_ref[...], 0.0), axis=1, keepdims=True)
    for cp in sends:
        cp.wait_recv()
    for b in range(nb):
        k = b % by
        s = so[b // by, k : k + 1, :] + to[b // by, k : k + 1, :]
        s = jnp.maximum(s, 0.2 * s)
        parts = [(pms[xx, b], pv[xx, b])] + [(rms[j, b], rv[j, b]) for j in range(NX - 1)]
        best = s
        for pm, _ in parts:
            best = jnp.maximum(best, pm[0:1])
        e = jnp.exp2(s - best)
        den = e
        total = e * fo[b].astype(jnp.float32)
        for pm, val in parts:
            e = jnp.exp2(pm[0:1] - best)
            den = den + e * pm[1:2]
            total = total + e * val.astype(jnp.float32)
        at = slice(b * LANES, (b + 1) * LANES)
        v = total / den + x_ref[:, at].astype(jnp.float32) + bias
        v = jnp.where(v > 0, v, jnp.exp2(jnp.minimum(v, 0.0) * LOG2E) - 1.0)
        out_ref[:, at] = v.astype(jnp.bfloat16)
    for cp in sends:
        cp.wait_send()


def local(node_feats, proj_weight, att_src, att_dst, out_bias, tile_rows, tile_cols, tile_masks):
    n = node_feats.shape[1]
    fin = proj_weight.shape[1]
    ny = fin // HD
    nb = n // LANES
    by = nb // ny
    ndp = NX * NZ * NC
    tiles = tile_rows.shape[0]
    vmem = pl.BlockSpec(memory_space=pltpu.VMEM)
    smem = pl.BlockSpec(memory_space=pltpu.SMEM)
    hbm = pl.BlockSpec(memory_space=pl.ANY)
    f32, i32, bf16 = jnp.float32, jnp.int32, jnp.bfloat16
    shape = jax.ShapeDtypeStruct
    dma = pltpu.SemaphoreType.DMA

    slots, codes = pl.pallas_call(
        functools.partial(prep_kernel, nb),
        out_shape=(shape((ndp, CAP, 4, LANES), i32), shape((ndp, 1, LANES), i32)),
        in_specs=[smem, smem, vmem],
        out_specs=(vmem, vmem),
        scratch_shapes=[pltpu.SMEM((ndp,), i32)],
        name="prep",
    )(tile_rows, tile_cols, tile_masks)

    ng = NZ * NC
    wr = HD + 16
    F, S, T4, M4, I4 = pl.pallas_call(
        functools.partial(gather_kernel, ny, nb),
        out_shape=(
            shape((ng * nb, HD, LANES), bf16),
            shape((ng, ny, by, LANES), f32),
            shape((NX, ny, by, LANES), f32),
            shape((NX, ndp, CAP, 4, LANES), i32),
            shape((NX, ndp, 1, LANES), i32),
        ),
        in_specs=[vmem] * 6,
        out_specs=(vmem,) * 5,
        scratch_shapes=[
            pltpu.VMEM((wr, fin), bf16),
            pltpu.VMEM((ny, wr, fin), bf16),
            pltpu.VMEM((fin, by * LANES), bf16),
            pltpu.VMEM((ny, by, HD, LANES), bf16),
            pltpu.VMEM((ny, by, LANES), f32),
            pltpu.VMEM((ny, by, LANES), f32),
            dma((19,)),
            dma((ny,)),
            dma((2, NZ // 2, ny)),
            dma((2, NZ // 2, ny)),
            dma((2, NZ // 2)),
            dma((2, NZ // 2)),
            dma((NZ,)),
            dma((NZ,)),
            dma((NZ,)),
            dma((NZ,)),
        ],
        compiler_params=pltpu.CompilerParams(collective_id=0, has_side_effects=True),
        name="gather",
    )(node_feats, proj_weight, att_src.reshape(1, HD), att_dst.reshape(1, HD), slots, codes)

    nrow = NX * nb
    nslot = NX * ndp * CAP
    chunks = max(1, nslot // LANES)
    pv, pms = pl.pallas_call(
        functools.partial(tile_kernel, nb),
        out_shape=(shape((nrow, HD, LANES), bf16), shape((nrow, 2, LANES), f32)),
        in_specs=[vmem] * 5,
        out_specs=(vmem, vmem),
        scratch_shapes=[
            pltpu.VMEM((max(1, ng * nb // LANES), LANES, LANES), f32),
            pltpu.SMEM((chunks + 1, 1, LANES), i32),
            pltpu.VMEM((nrow, HD + 8, LANES), f32),
            pltpu.VMEM((nrow, 1, LANES), f32),
            pltpu.VMEM((chunks + 1, 1, LANES), i32),
            dma(()),
        ],
        name="tiles",
    )(
        F,
        S.reshape(ng * nb, LANES),
        T4.reshape(nrow, 1, LANES),
        M4.reshape(nslot, 4, LANES),
        I4.reshape(NX * ndp, LANES),
    )

    return pl.pallas_call(
        functools.partial(merge_kernel, nb),
        out_shape=shape((HD, n), bf16),
        in_specs=[hbm, hbm, hbm, vmem, vmem, vmem, vmem],
        out_specs=vmem,
        scratch_shapes=[
            pltpu.VMEM((NX - 1, nb, HD, LANES), bf16),
            pltpu.VMEM((NX - 1, nb, 2, LANES), f32),
            pltpu.VMEM((nb, HD, LANES), bf16),
            pltpu.VMEM((ny, by, LANES), f32),
            pltpu.VMEM((ny, by, LANES), f32),
            dma((3,)),
            dma((NX - 1,)),
            dma((NX - 1,)),
            dma((NX - 1,)),
            dma((NX - 1,)),
        ],
        compiler_params=pltpu.CompilerParams(collective_id=1, has_side_effects=True),
        name="merge",
    )(
        F, S, T4, node_feats,
        jnp.pad(out_bias, (0, LANES - HD)).reshape(1, LANES),
        pv.reshape(NX, nb, HD, LANES),
        pms.reshape(NX, nb, 2, LANES),
    )


def solution(mesh):
    return jax.shard_map(
        local,
        mesh=mesh,
        in_specs=(
            P("mp", "dp"),
            P("mp", None),
            P("mp"),
            P("mp"),
            P("mp"),
            P("dp"),
            P("dp"),
            P("dp", None, None),
        ),
        out_specs=P("mp", "dp"),
        check_vma=False,
    )
```

time: 218 us -> 77.2 us (0.35)
  waiting for transfers between devices: 126 us -> 0 us
  Pallas kernels: 0 us -> 74.5 us
  starting transfers between devices: 37.6 us -> 0 us
  other arithmetic: 25.7 us -> 0 us
  local copies, waits for them, and re-layouts: 25.2 us -> 2.11 us
    all_to_all x5 -> x0, waiting for transfers between devices: 126 us -> none  [the longest x1 55.2 us: side_by_side_2(): lax.all_to_all(both, axis, split_axis=split_dim, concat_axis=concat_dim,...]
    pallas_call x0 -> x4, Pallas kernels: none -> 74.5 us  [the longest x1 51.3 us: local(): pl.pallas_call(functools.partial(gather_kernel, ny, nb), out_shape=(shape...]
    all_to_all x5 -> x0, starting transfers between devices: 37.6 us -> none  [the longest x2 19.4 us: side_by_side(): lax.all_to_all(both, axis, split_axis=split_dim, concat_axis=concat_dim,...]
    gather x13 -> x0, local copies, waits for them, and re-layouts: 11.7 us -> none  [the longest x2 4.5 us: local(): jnp.take(values, source_tile, axis=0)]
    scatter-add x2 -> x0, other arithmetic: 7.17 us -> none  [the longest x1 5.9 us: local(): summed = (self_weight[:, :, None, :] * feat_blocks.astype(jnp.float32)).a...]
    select_n x17 -> x0, other arithmetic: 5.31 us -> none  [the longest x1 2.36 us: local(): jnp.where(filled[:, None, None, None], jnp.take(values, source_tile, axis...]
    another operation x2 -> x0, local copies, waits for them, and re-layouts: 4.02 us -> none  [the longest x1 4.02 us: local(): got_values = got_values.reshape(slot_count, local_heads, HD, tile_size)]
    concatenate x3 -> x0, other arithmetic: 3.64 us -> none  [the longest x1 2.22 us: side_by_side_2(): both = jnp.concatenate(columns, axis=along)]
  transfers between devices with their start and end apart: 5 -> 0, of which waited for: 5 -> 0; matrix products, arithmetic and copies ran while one was open for 3% -> 0% of each run, Pallas kernels for 0% -> 0%
where the time goes in v1:
time: 77.2 us; the launch traced here: 76.6 us
  Pallas kernels  74.5 us (97%)
  local copies, waits for them, and re-layouts  2.11 us (3%)
    pallas_call x1, Pallas kernels, local(): pl.pallas_call(functools.partial(gather_kernel, ny, nb), out_shape=(shape...  51.3 us
    pallas_call x1, Pallas kernels, local(): pl.pallas_call(functools.partial(merge_kernel, nb), out_shape=shape((HD,...  12.6 us
    pallas_call x1, Pallas kernels, local(): pl.pallas_call(functools.partial(tile_kernel, nb), out_shape=(shape((nrow...  8.07 us
    pallas_call x1, Pallas kernels, local(): pl.pallas_call(functools.partial(prep_kernel, nb), out_shape=(shape((ndp,...  2.47 us
    unnamed x3, local copies, waits for them, and re-layouts  1.57 us

profile of v1, /device:TPU:1, one launch (start us, length us, event | category | flops | bytes accessed | tf_op | source)
XLA Modules:
  0.0 76.6 jit_solution(6935668650043345083)
XLA Ops:
  0.0 0.0 copy-start
  0.0 2.5 %prep.1 = (s32[64,2,4,128]{3,2,1,0:T(4,128)}, s32[64,1,128]{2,1,0:T(1,128)}) custom-call(s32[32]{0:T(128)} %rows_ref.1, s32[32]{0:T(128)} %cols_ref.1, s32[32,4,128]{2,1,0:T(4,128)} %mask_ref.1), custom_call_target="tpu_custom_call" | custom-call | tf_op jit(solution)/shard_map/prep/pallas_call | solution.py:441
  2.5 51.3 %gather.1 = (bf16[256,32,128]{2,1,0:T(8,128)(2,1)}, f32[16,8,2,128]{3,2,1,0:T(2,128)}, f32[4,8,2,128]{3,2,1,0:T(2,128)}, s32[4,64,2,4,128]{4,3,2,1,0:T(4,128)}, s32[4,64,1,128]{3,2,1,0:T(1,128)}) custom-call(bf16[32,2048]{1,0:T(8,128)(2,1)} %x_ref.3, bf16[32,256]{1,0:T(8,128)(2,1)} %w_ref.1, f32[1,32]{1,0:T(1,128)} %bitcast.16, f32[1,32]{1,0:T(1,128)} %bitcast.17, ...), custom_call_target="tpu_custom_call" | custom-call | tf_op jit(solution)/shard_map/gather/pallas_call | solution.py:452
  53.8 8.1 %tiles.1 = (bf16[64,32,128]{2,1,0:T(8,128)(2,1)}, f32[64,2,128]{2,1,0:T(2,128)}) custom-call(bf16[256,32,128]{2,1,0:T(8,128)(2,1)} %get-tuple-element.16.F, f32[256,128]{1,0:T(8,128)} %bitcast.12, f32[64,1,128]{2,1,0:T(1,128)} %bitcast.13, s32[512,4,128]{2,1,0:T(4,128)} %bitcast.10, s32[256,128]{1,0:T(8,128)} %bitcast.14), custom_call_target="tpu_custom_call" | custom-call | tf_op jit(solution)/shard_map/tiles/pallas_call | solution.py:488
  61.9 0.0 copy-done
  61.9 0.5 pad_bitcast_fusion.b_ref
  62.4 12.6 %merge.1 = bf16[32,2048]{1,0:T(8,128)(2,1)} custom-call(bf16[256,32,128]{2,1,0:T(8,128)(2,1)} %get-tuple-element.16.F, f32[16,8,2,128]{3,2,1,0:T(2,128)} %get-tuple-element.17.S, f32[4,8,2,128]{3,2,1,0:T(2,128)} %get-tuple-element.18.T4, bf16[32,2048]{1,0:T(8,128)(2,1)} %x_ref.3, f32[1,128]{1,0:T(1,128)} %pad_bitcast_fusion.b_ref, ...), custom_call_target="tpu_custom_call" | custom-call | tf_op jit(solution)/shard_map/merge/pallas_call | solution.py:510
  75.0 1.6 %copy.10 = bf16[32,2048]{1,0:T(8,128)(2,1)} copy(bf16[32,2048]{1,0:T(8,128)(2,1)} %merge.1) | data formatting | bytes 262144
Async XLA Ops:
  0.0 61.9 %copy-start = (f32[32]{0:T(128)S(1)}, f32[32]{0:T(128)}, u32[]{:S(2)}) copy-start(f32[32]{0:T(128)} %param.12) | copy-start | bytes 388

commit v2 on v1

--- a/solution.py
+++ b/solution.py
@@ -16,6 +16,7 @@
 NX, NZ, NC = 4, 8, 2
 CAP = 2
 UNROLL = 4
+ROOM = 24 * 2**20
 
 
 def split3(v):
@@ -32,6 +33,14 @@
     for i, part in enumerate(parts):
         out = jnp.where(at == i, part, out)
     return out
+
+
+def on_chip(shape, dtype):
+    return pltpu.VMEM(shape, dtype)
+
+
+def held(x):
+    return pltpu.with_memory_space_constraint(x, pltpu.VMEM)
 
 
 def wait_bytes(ref, sem):
@@ -364,62 +373,83 @@
     lax.fori_loop(0, nrow, put, 0)
 
 
-def merge_kernel(nb, F, S, T4, x_ref, b_ref, pv, pms, out_ref, rv, rms, fo, so, to, loc, s_v, r_v, s_m, r_m):
+def merge_kernel(
+    nb, F, S, T4, x_ref, b_ref, pv, pms, out_ref,
+    rv, rms, hv, hms, total_ref, state_ref, s_v, r_v, s_m, r_m,
+):
     dp = lax.axis_index("dp")
     c = dp % NC
     z = (dp // NC) % NZ
     xx = dp // (NC * NZ)
     own = z * NC + c
-    by = so.shape[1]
-    copies = [
-        pltpu.make_async_copy(F.at[pl.ds(own * nb, nb)], fo, loc.at[0]),
-        pltpu.make_async_copy(S.at[own], so, loc.at[1]),
-        pltpu.make_async_copy(T4.at[xx], to, loc.at[2]),
-    ]
-    for cp in copies:
-        cp.start()
+    by = S.shape[2]
+    half = nb // 2
+    up, opp, down = [lax.rem(xx + j, NX) for j in (1, 2, 3)]
+
+    def dev(p):
+        return {"dp": (p * NZ + z) * NC + c}
+
     barrier = pltpu.get_barrier_semaphore()
-    peers = [lax.rem(xx + j, NX) for j in range(1, NX)]
-    for p in peers:
-        pl.semaphore_signal(barrier, inc=1, device_id={"dp": (p * NZ + z) * NC + c}, device_id_type=MESH)
-    pl.semaphore_wait(barrier, NX - 1)
-    sends = []
-    for j, p in enumerate(peers):
-        at = {"dp": (p * NZ + z) * NC + c}
-        for src, dst, ssem, rsem in ((pms, rms, s_m, r_m), (pv, rv, s_v, r_v)):
+    for p in (up, down):
+        pl.semaphore_signal(barrier, inc=1, device_id=dev(p), device_id_type=MESH)
+    pl.semaphore_wait(barrier, 2)
+
+    def both(i, src_v, dst_v, src_m, dst_m, p):
+        out = []
+        for src, dst, ssem, rsem in ((src_m, dst_m, s_m, r_m), (src_v, dst_v, s_v, r_v)):
             cp = pltpu.make_async_remote_copy(
-                src_ref=src.at[p], dst_ref=dst.at[j], send_sem=ssem.at[j], recv_sem=rsem.at[j],
-                device_id=at, device_id_type=MESH,
+                src_ref=src, dst_ref=dst, send_sem=ssem.at[i], recv_sem=rsem.at[i],
+                device_id=dev(p), device_id_type=MESH,
             )
             cp.start()
-            sends.append(cp)
-    for cp in copies:
-        cp.wait()
-    rowi = lax.broadcasted_iota(jnp.int32, (HD, LANES), 0)
-    lanei = lax.broadcasted_iota(jnp.int32, (HD, LANES), 1)
+            out.append(cp)
+        return out
+
+    lo, hi = pl.ds(0, half), pl.ds(half, half)
+    via_up = both(0, pv.at[opp, lo], hv.at[0], pms.at[opp, lo], hms.at[0], up)
+    via_down = both(1, pv.at[opp, hi], hv.at[1], pms.at[opp, hi], hms.at[1], down)
+    to_up = both(2, pv.at[up], rv.at[0], pms.at[up], rms.at[0], up)
+    to_down = both(3, pv.at[down], rv.at[1], pms.at[down], rms.at[1], down)
+
+    rowi = lax.broadcasted_iota(jnp.int32, (HD, HD), 0)
+    lanei = lax.broadcasted_iota(jnp.int32, (HD, HD), 1)
     bias = jnp.sum(jnp.where(rowi == lanei, b_ref[...], 0.0), axis=1, keepdims=True)
-    for cp in sends:
+
+    for cp in via_up:
+        cp.wait_recv()
+    on_up = both(4, hv.at[0], rv.at[2, lo], hms.at[0], rms.at[2, lo], up)
+    for cp in via_down:
+        cp.wait_recv()
+    on_down = both(5, hv.at[1], rv.at[2, hi], hms.at[1], rms.at[2, hi], down)
+    for cp in to_up + to_down:
+        cp.wait_recv()
+
+    def join(best, den, total, pm, val):
+        new = jnp.maximum(best, pm[0:1])
+        old_e = jnp.exp2(best - new)
+        e = jnp.exp2(pm[0:1] - new)
+        return new, den * old_e + e * pm[1:2], total * old_e + e * val.astype(jnp.float32)
+
+    for b in range(nb):
+        k = b % by
+        s = S[own, b // by, k : k + 1, :] + T4[xx, b // by, k : k + 1, :]
+        best = jnp.maximum(s, 0.2 * s)
+        den = jnp.ones_like(best)
+        total = F[own * nb + b].astype(jnp.float32)
+        for pm, val in ((pms[xx, b], pv[xx, b]), (rms[0, b], rv[0, b]), (rms[1, b], rv[1, b])):
+            best, den, total = join(best, den, total, pm, val)
+        total_ref[b] = total
+        state_ref[b, 0:1, :] = best
+        state_ref[b, 1:2, :] = den
+    for cp in on_up + on_down:
         cp.wait_recv()
     for b in range(nb):
-        k = b % by
-        s = so[b // by, k : k + 1, :] + to[b // by, k : k + 1, :]
-        s = jnp.maximum(s, 0.2 * s)
-        parts = [(pms[xx, b], pv[xx, b])] + [(rms[j, b], rv[j, b]) for j in range(NX - 1)]
-        best = s
-        for pm, _ in parts:
-            best = jnp.maximum(best, pm[0:1])
-        e = jnp.exp2(s - best)
-        den = e
-        total = e * fo[b].astype(jnp.float32)
-        for pm, val in parts:
-            e = jnp.exp2(pm[0:1] - best)
-            den = den + e * pm[1:2]
-            total = total + e * val.astype(jnp.float32)
+        best, den, total = join(state_ref[b, 0:1, :], state_ref[b, 1:2, :], total_ref[b], rms[2, b], rv[2, b])
         at = slice(b * LANES, (b + 1) * LANES)
         v = total / den + x_ref[:, at].astype(jnp.float32) + bias
         v = jnp.where(v > 0, v, jnp.exp2(jnp.minimum(v, 0.0) * LOG2E) - 1.0)
         out_ref[:, at] = v.astype(jnp.bfloat16)
-    for cp in sends:
+    for cp in via_up + via_down + to_up + to_down + on_up + on_down:
         cp.wait_send()
 
 
@@ -433,17 +463,17 @@
     tiles = tile_rows.shape[0]
     vmem = pl.BlockSpec(memory_space=pltpu.VMEM)
     smem = pl.BlockSpec(memory_space=pltpu.SMEM)
-    hbm = pl.BlockSpec(memory_space=pl.ANY)
     f32, i32, bf16 = jnp.float32, jnp.int32, jnp.bfloat16
     shape = jax.ShapeDtypeStruct
     dma = pltpu.SemaphoreType.DMA
 
     slots, codes = pl.pallas_call(
         functools.partial(prep_kernel, nb),
-        out_shape=(shape((ndp, CAP, 4, LANES), i32), shape((ndp, 1, LANES), i32)),
+        out_shape=(on_chip((ndp, CAP, 4, LANES), i32), on_chip((ndp, 1, LANES), i32)),
         in_specs=[smem, smem, vmem],
         out_specs=(vmem, vmem),
         scratch_shapes=[pltpu.SMEM((ndp,), i32)],
+        compiler_params=pltpu.CompilerParams(vmem_limit_bytes=ROOM),
         name="prep",
     )(tile_rows, tile_cols, tile_masks)
 
@@ -452,11 +482,11 @@
     F, S, T4, M4, I4 = pl.pallas_call(
         functools.partial(gather_kernel, ny, nb),
         out_shape=(
-            shape((ng * nb, HD, LANES), bf16),
-            shape((ng, ny, by, LANES), f32),
-            shape((NX, ny, by, LANES), f32),
-            shape((NX, ndp, CAP, 4, LANES), i32),
-            shape((NX, ndp, 1, LANES), i32),
+            on_chip((ng * nb, HD, LANES), bf16),
+            on_chip((ng, ny, by, LANES), f32),
+            on_chip((NX, ny, by, LANES), f32),
+            on_chip((NX, ndp, CAP, 4, LANES), i32),
+            on_chip((NX, ndp, 1, LANES), i32),
         ),
         in_specs=[vmem] * 6,
         out_specs=(vmem,) * 5,
@@ -478,16 +508,16 @@
             dma((NZ,)),
             dma((NZ,)),
         ],
-        compiler_params=pltpu.CompilerParams(collective_id=0, has_side_effects=True),
+        compiler_params=pltpu.CompilerParams(collective_id=0, has_side_effects=True, vmem_limit_bytes=ROOM),
         name="gather",
-    )(node_feats, proj_weight, att_src.reshape(1, HD), att_dst.reshape(1, HD), slots, codes)
+    )(node_feats, proj_weight, att_src.reshape(1, HD), att_dst.reshape(1, HD), held(slots), held(codes))
 
     nrow = NX * nb
     nslot = NX * ndp * CAP
     chunks = max(1, nslot // LANES)
     pv, pms = pl.pallas_call(
         functools.partial(tile_kernel, nb),
-        out_shape=(shape((nrow, HD, LANES), bf16), shape((nrow, 2, LANES), f32)),
+        out_shape=(on_chip((nrow, HD, LANES), bf16), on_chip((nrow, 2, LANES), f32)),
         in_specs=[vmem] * 5,
         out_specs=(vmem, vmem),
         scratch_shapes=[
@@ -498,39 +528,39 @@
             pltpu.VMEM((chunks + 1, 1, LANES), i32),
             dma(()),
         ],
+        compiler_params=pltpu.CompilerParams(vmem_limit_bytes=ROOM),
         name="tiles",
     )(
-        F,
-        S.reshape(ng * nb, LANES),
-        T4.reshape(nrow, 1, LANES),
-        M4.reshape(nslot, 4, LANES),
-        I4.reshape(NX * ndp, LANES),
+        held(F),
+        held(S.reshape(ng * nb, LANES)),
+        held(T4.reshape(nrow, 1, LANES)),
+        held(M4.reshape(nslot, 4, LANES)),
+        held(I4.reshape(NX * ndp, LANES)),
     )
 
     return pl.pallas_call(
         functools.partial(merge_kernel, nb),
-        out_shape=shape((HD, n), bf16),
-        in_specs=[hbm, hbm, hbm, vmem, vmem, vmem, vmem],
+        out_shape=on_chip((HD, n), bf16),
+        in_specs=[vmem] * 7,
         out_specs=vmem,
         scratch_shapes=[
-            pltpu.VMEM((NX - 1, nb, HD, LANES), bf16),
-            pltpu.VMEM((NX - 1, nb, 2, LANES), f32),
-            pltpu.VMEM((nb, HD, LANES), bf16),
-            pltpu.VMEM((ny, by, LANES), f32),
-            pltpu.VMEM((ny, by, LANES), f32),
-            dma((3,)),
-            dma((NX - 1,)),
-            dma((NX - 1,)),
-            dma((NX - 1,)),
-            dma((NX - 1,)),
+            pltpu.VMEM((3, nb, HD, LANES), bf16),
+            pltpu.VMEM((3, nb, 2, LANES), f32),
+            pltpu.VMEM((2, nb // 2, HD, LANES), bf16),
+            pltpu.VMEM((2, nb // 2, 2, LANES), f32),
+            pltpu.VMEM((nb, HD, LANES), f32),
+            pltpu.VMEM((nb, 2, LANES), f32),
+            dma((6,)),
+            dma((6,)),
+            dma((6,)),
+            dma((6,)),
         ],
-        compiler_params=pltpu.CompilerParams(collective_id=1, has_side_effects=True),
+        compiler_params=pltpu.CompilerParams(collective_id=1, has_side_effects=True, vmem_limit_bytes=ROOM),
         name="merge",
     )(
-        F, S, T4, node_feats,
-        jnp.pad(out_bias, (0, LANES - HD)).reshape(1, LANES),
-        pv.reshape(NX, nb, HD, LANES),
-        pms.reshape(NX, nb, 2, LANES),
+        held(F), held(S), held(T4), node_feats, out_bias.reshape(1, HD),
+        held(pv.reshape(NX, nb, HD, LANES)),
+        held(pms.reshape(NX, nb, 2, LANES)),
     )
 
 

time: 77.2 us -> 71.4 us (0.925)
  Pallas kernels: 74.5 us -> 64.9 us
  local copies, waits for them, and re-layouts: 2.11 us -> 5.75 us
    pallas_call x4, Pallas kernels: 74.5 us -> 64.9 us  [the longest x1 48.7 us: local(): pl.pallas_call(functools.partial(gather_kernel, ny, nb), out_shape=(on_ch...]
    unnamed x3 -> x17, local copies, waits for them, and re-layouts: 1.57 us -> 5.75 us
where the time goes in v2:
time: 71.4 us; the launch traced here: 70.7 us
  Pallas kernels  64.9 us (91%)
  local copies, waits for them, and re-layouts  5.75 us (8%)
    pallas_call x1, Pallas kernels, local(): pl.pallas_call(functools.partial(gather_kernel, ny, nb), out_shape=(on_ch...  48.7 us
    pallas_call x1, Pallas kernels, local(): pl.pallas_call(functools.partial(merge_kernel, nb), out_shape=on_chip((HD...  10.2 us
    unnamed x17, local copies, waits for them, and re-layouts  5.75 us
    pallas_call x1, Pallas kernels, local(): pl.pallas_call(functools.partial(tile_kernel, nb), out_shape=(on_chip((nr...  4.53 us
    pallas_call x1, Pallas kernels, local(): pl.pallas_call(functools.partial(prep_kernel, nb), out_shape=(on_chip((nd...  1.43 us

profile of v2, /device:TPU:1, one launch (start us, length us, event | category | flops | bytes accessed | tf_op | source)
XLA Modules:
  0.0 70.7 jit_solution(10206618478305995666)
XLA Ops:
  0.0 0.0 copy-start.7
  0.0 0.0 copy-start.1
  0.0 0.9 %copy-done.1 = s32[32,4,128]{2,1,0:T(4,128)S(1)} copy-done((s32[32,4,128]{2,1,0:T(4,128)S(1)}, s32[32,4,128]{2,1,0:T(4,128)}, u32[]{:S(2)}) %copy-start.1) | copy-done | bytes 65560
  0.9 0.0 copy-start.3
  0.9 0.7 copy-done.3
  1.5 0.0 copy-start.4
  1.5 0.7 copy-done.4
  2.2 1.4 %prep.1 = (s32[64,2,4,128]{3,2,1,0:T(4,128)S(1)}, s32[64,1,128]{2,1,0:T(1,128)S(1)}) custom-call(s32[32]{0:T(128)S(1)} %copy-done.3, s32[32]{0:T(128)S(1)} %copy-done.4, s32[32,4,128]{2,1,0:T(4,128)S(1)} %copy-done.1), custom_call_target="tpu_custom_call" | custom-call | tf_op jit(solution)/shard_map/prep/pallas_call | solution.py:470
  3.6 0.0 copy-start
  3.6 0.9 %copy-done = bf16[32,2048]{1,0:T(8,128)(2,1)S(1)} copy-done((bf16[32,2048]{1,0:T(8,128)(2,1)S(1)}, bf16[32,2048]{1,0:T(8,128)(2,1)}, u32[]{:S(2)}) %copy-start) | copy-done | bytes 131096
  4.5 0.0 copy-start.2
  4.5 0.7 %copy-done.2 = bf16[32,256]{1,0:T(8,128)(2,1)S(1)} copy-done((bf16[32,256]{1,0:T(8,128)(2,1)S(1)}, bf16[32,256]{1,0:T(8,128)(2,1)}, u32[]{:S(2)}) %copy-start.2) | copy-done | bytes 16408
  5.2 0.0 copy-start.5
  5.2 0.7 copy-done.5
  5.9 0.0 copy-start.6
  5.9 0.7 copy-done.6
  6.5 48.7 %gather.1 = (bf16[256,32,128]{2,1,0:T(8,128)(2,1)S(1)}, f32[16,8,2,128]{3,2,1,0:T(2,128)S(1)}, f32[4,8,2,128]{3,2,1,0:T(2,128)S(1)}, s32[4,64,2,4,128]{4,3,2,1,0:T(4,128)S(1)}, s32[4,64,1,128]{3,2,1,0:T(1,128)S(1)}) custom-call(bf16[32,2048]{1,0:T(8,128)(2,1)S(1)} %copy-done, bf16[32,256]{1,0:T(8,128)(2,1)S(1)} %copy-done.2, f32[1,32]{1,0:T(1,128)S(1)} %bitcast.15, ...), custom_call_target="tpu_custom_call" | custom-call | tf_op jit(solution)/shard_map/gather/pallas_call | solution.py:482
  55.2 4.5 %tiles.1 = (bf16[64,32,128]{2,1,0:T(8,128)(2,1)S(1)}, f32[64,2,128]{2,1,0:T(2,128)S(1)}) custom-call(bf16[256,32,128]{2,1,0:T(8,128)(2,1)S(1)} %get-tuple-element.16.F, f32[256,128]{1,0:T(8,128)S(1)} %bitcast.11, f32[64,1,128]{2,1,0:T(1,128)S(1)} %bitcast.12, s32[512,4,128]{2,1,0:T(4,128)S(1)} %bitcast.9, s32[256,128]{1,0:T(8,128)S(1)} %bitcast.13), custom_call_target="tpu_custom_call" | custom-call | tf_op jit(solution)/shard_map/tiles/pallas_call | solution.py:518
  59.8 0.0 copy-done.7
  59.8 10.2 %merge.1 = bf16[32,2048]{1,0:T(8,128)(2,1)S(1)} custom-call(bf16[256,32,128]{2,1,0:T(8,128)(2,1)S(1)} %get-tuple-element.16.F, f32[16,8,2,128]{3,2,1,0:T(2,128)S(1)} %get-tuple-element.17.S, f32[4,8,2,128]{3,2,1,0:T(2,128)S(1)} %get-tuple-element.18.T4, bf16[32,2048]{1,0:T(8,128)(2,1)S(1)} %copy-done, f32[1,32]{1,0:T(1,128)S(1)} %bitcast.17, ...), custom_call_target="tpu_custom_call" | custom-call | tf_op jit(solution)/shard_map/merge/pallas_call | solution.py:541
  70.0 0.7 copy.10
Async XLA Ops:
  0.0 59.8 %copy-start.7 = (f32[32]{0:T(128)S(1)}, f32[32]{0:T(128)}, u32[]{:S(2)}) copy-start(f32[32]{0:T(128)} %param.12) | copy-start | bytes 388
  0.0 0.9 %copy-start.1 = (s32[32,4,128]{2,1,0:T(4,128)S(1)}, s32[32,4,128]{2,1,0:T(4,128)}, u32[]{:S(2)}) copy-start(s32[32,4,128]{2,1,0:T(4,128)} %mask_ref.1) | copy-start | bytes 196612
  0.9 0.7 copy-start.3
  1.5 0.7 copy-start.4
  3.6 0.9 %copy-start = (bf16[32,2048]{1,0:T(8,128)(2,1)S(1)}, bf16[32,2048]{1,0:T(8,128)(2,1)}, u32[]{:S(2)}) copy-start(bf16[32,2048]{1,0:T(8,128)(2,1)} %x_ref.3) | copy-start | bytes 393220
  4.5 0.7 %copy-start.2 = (bf16[32,256]{1,0:T(8,128)(2,1)S(1)}, bf16[32,256]{1,0:T(8,128)(2,1)}, u32[]{:S(2)}) copy-start(bf16[32,256]{1,0:T(8,128)(2,1)} %w_ref.1) | copy-start | bytes 49156
  5.2 0.7 copy-start.5
  5.9 0.7 copy-start.6
